TPU v7x, 128 devices: a whole 4x4x4 slice. The times are simulated.
128 devices in a mesh: seq: 32 (over z, x, core), group: 4 (over y).
Axes of the slice: x: 4, y: 4, z: 4, core: 2. Of those that a mesh axis runs over, the one named last changes fastest.
Arguments:
- new_queries: bfloat16 [32, 8, 8, 128], P('seq', 'group'), may hold values from -6 to 6
- stored_keys: bfloat16 [32, 8, 16384, 128], P(None, 'group', 'seq'), may hold values from -6 to 6
- stored_values: bfloat16 [32, 8, 16384, 128], P(None, 'group', 'seq'), may hold values from -6 to 6
- used_length: int32 [32], replicated, may hold values from 8192 to 16384
- out_weight: bfloat16 [8, 8, 128, 5120], P('group'), may hold values from -0.0625 to 0.0625
Outputs:
- token_out: bfloat16 [32, 5120], P('seq', 'group')
All inputs are finite; a program needn't handle non-finite values.
Results may differ from a plain program's by a relative error of at most 0.0025.
Values may be sent and summed in bfloat16 or wider, within the bound.
No kernel may reach another device: no remote copies, remote signals or barrier semaphores. Data moves between devices by JAX's collectives and lax.ppermute only.
A program may use at most 128 MiB of HBM per device.

v0:
```python
import jax
import jax.numpy as jnp
from jax import lax
from jax.sharding import PartitionSpec as P

HEAD_SIZE = 128


def per_device(new_queries, stored_keys, stored_values, used_length, out_weight):
    all_queries = lax.all_gather(new_queries, "seq", axis=0, tiled=True)
    logit = jnp.einsum(
        "bkgd,bktd->bkgt", all_queries, stored_keys, preferred_element_type=jnp.float32
    ) * HEAD_SIZE ** (-0.5)
    positions = lax.axis_index("seq") * stored_keys.shape[2] + jnp.arange(stored_keys.shape[2])
    filled = positions[None, :] < used_length[:, None]
    logit = jnp.where(filled[:, None, None, :], logit, -1e30)
    top = jnp.max(logit, axis=-1)
    part = jnp.where(filled[:, None, None, :], jnp.exp(logit - top[..., None]), 0.0)
    weight_sum = jnp.sum(part, axis=-1)
    read_sum = jnp.einsum(
        "bkgt,bktd->bkgd", part, stored_values.astype(jnp.float32), precision=lax.Precision.HIGHEST
    )
    tops, sums, parts = (
        lax.all_to_all(top[None], "seq", split_axis=1, concat_axis=0, tiled=True),
        lax.all_to_all(weight_sum[None], "seq", split_axis=1, concat_axis=0, tiled=True),
        lax.all_to_all(read_sum[None], "seq", split_axis=1, concat_axis=0, tiled=True),
    )
    best = jnp.max(tops, axis=0)
    scale = jnp.exp(tops - best)
    weight_own = jnp.sum(sums * scale, axis=0)
    read_own = jnp.sum(parts * scale[..., None], axis=0)
    read = (read_own / weight_own[..., None]).astype(jnp.bfloat16)
    term = jnp.einsum("bkgd,kgdm->bm", read, out_weight, preferred_element_type=jnp.float32)
    token_out = lax.psum_scatter(term, "group", scatter_dimension=1, tiled=True).astype(
        jnp.bfloat16
    )
    return token_out


def solution(mesh):
    in_specs = (
        P("seq", "group", None, None),
        P(None, "group", "seq", None),
        P(None, "group", "seq", None),
        P(),
        P("group", None, None, None),
    )
    out_specs = P("seq", "group")
    return jax.shard_map(
        per_device, mesh=mesh, in_specs=in_specs, out_specs=out_specs, check_vma=False
    )
```

profile of v0, /device:TPU:1, one launch (start us, length us, event | category | flops | bytes accessed | tf_op | source)
XLA Modules:
  0.0 134.0 jit_solution(4825849419178507323)
XLA Ops:
  6.5 27.3 %all_gather.3 = bf16[32,2,8,128]{3,2,1,0:T(8,128)(2,1)S(1)} all-gather(bf16[1,2,8,128]{3,2,1,0:T(8,128)(2,1)} %param.5), channel_id=1, replica_groups=mesh['seq'=32,'group'=4] {'seq'}, dimensions={0}, use_global_device_ids=true | all-gather | bytes 135168 | tf_op jit(solution)/shard_map/all_gather | solution.py:10
  33.9 0.7 broadcast_compare_fusion
  34.6 6.4 %fusion.18 = (f32[32,2,8]{2,1,0:T(2,128)}, f32[32,2,8,512]{3,2,1,0:T(8,128)S(1)}) fusion(bf16[32,2,8,128]{3,2,1,0:T(8,128)(2,1)S(1)} %all_gather.3, bf16[32,2,512,128]{3,2,1,0:T(8,128)(2,1)} %param.6, pred[32,512]{1,0:T(8,128)(4,1)S(1)} %broadcast_compare_fusion), kind=kOutput, calls=%fused_computation.25 | convolution fusion | flops 67894784 | bytes 9586688 | tf_op jit(solution)/shard_map/bkgd,bktd->bkgt/dot_general | solution.py:11
  41.0 4.9 %all-to-all-start.1 = ((f32[1,32,2,8]{3,2,0,1:T(2,128)}), f32[1,32,2,8]{3,2,0,1:T(2,128)S(1)}, u32[]{:S(2)}, u32[]{:S(2)}) async-start(f32[1,32,2,8]{3,2,0,1:T(2,128)} %bitcast.3), calls=%async_computation.1 | async-start | bytes 65536 | tf_op jit(solution)/shard_map/all_to_all | solution.py:24
  45.9 1.8 %fusion.6 = f32[32,2,8]{2,1,0:T(2,128)} fusion(f32[32,2,8,512]{3,2,1,0:T(8,128)S(1)} %get-tuple-element.6, f32[32,2,8]{2,1,0:T(2,128)} %get-tuple-element.5, pred[32,512]{1,0:T(8,128)(4,1)S(1)} %broadcast_compare_fusion), kind=kLoop, calls=%fused_computation.7 | loop fusion | flops 785920 | bytes 1069056 | tf_op jit(solution)/shard_map/reduce_sum | solution.py:19
  47.6 5.5 %all-to-all-done.1 = f32[1,32,2,8]{3,2,0,1:T(2,128)S(1)} async-done(((f32[1,32,2,8]{3,2,0,1:T(2,128)}), f32[1,32,2,8]{3,2,0,1:T(2,128)S(1)}, u32[]{:S(2)}, u32[]{:S(2)}) %all-to-all-start.1) | async-done | bytes 2080 | tf_op jit(solution)/shard_map/all_to_all | solution.py:24
  53.1 3.9 %all-to-all-start.2 = ((f32[1,32,2,8]{3,2,0,1:T(2,128)}), f32[1,32,2,8]{3,2,0,1:T(2,128)S(1)}, u32[]{:S(2)}, u32[]{:S(2)}) async-start(f32[1,32,2,8]{3,2,0,1:T(2,128)} %bitcast.5), calls=%async_computation.2 | async-start | bytes 65536 | tf_op jit(solution)/shard_map/all_to_all | solution.py:25
  57.0 6.5 %convolution_bitcast_fusion = f32[1,32,2,8,128]{4,3,2,0,1:T(8,128)} fusion(bf16[32,2,512,128]{3,2,1,0:T(8,128)(2,1)} %param.7, f32[32,2,8,512]{3,2,1,0:T(8,128)S(1)} %get-tuple-element.6, f32[32,2,8]{2,1,0:T(2,128)} %get-tuple-element.5, pred[32,512]{1,0:T(8,128)(4,1)S(1)} %broadcast_compare_fusion), kind=kOutput, calls=%fused_computation.5 | convolution fusion | flops 403177472 | bytes 9717760 | tf_op jit(solution)/shard_map/bkgt,bktd->bkgd/dot_general | solution.py:20
  63.6 0.8 all-to-all-done.2
  64.4 6.7 %all-to-all-start = ((f32[1,32,2,8,128]{4,3,2,0,1:T(8,128)}), f32[1,32,2,8,128]{4,3,2,0,1:T(8,128)S(1)}, u32[]{:S(2)}, u32[]{:S(2)}) async-start(f32[1,32,2,8,128]{4,3,2,0,1:T(8,128)} %convolution_bitcast_fusion), calls=%async_computation | async-start | bytes 524288 | tf_op jit(solution)/shard_map/all_to_all | solution.py:26
  71.1 0.0 reduce-scatter.4.cloned.1.call-start
  71.1 0.1 fusion.14
  71.2 8.7 %all-to-all-done = f32[1,32,2,8,128]{4,3,2,0,1:T(8,128)S(1)} async-done(((f32[1,32,2,8,128]{4,3,2,0,1:T(8,128)}), f32[1,32,2,8,128]{4,3,2,0,1:T(8,128)S(1)}, u32[]{:S(2)}, u32[]{:S(2)}) %all-to-all-start) | async-done | bytes 262176 | tf_op jit(solution)/shard_map/all_to_all | solution.py:26
  80.0 0.1 fusion.10
  80.1 0.1 fusion.16
  80.2 13.4 %fusion.2 = f32[5120,1]{1,0:T(8,128)} fusion(bf16[2,8,128,5120]{3,2,1,0:T(8,128)(2,1)} %param.9, bf16[2,8,128,1]{2,1,0,3:T(8,128)(2,1)S(1)} %fusion.16), kind=kOutput, calls=%fused_computation.2 | convolution fusion | flops 20971520 | bytes 20996096 | tf_op jit(solution)/shard_map/bkgd,kgdm->bm/dot_general | solution.py:33
  93.6 0.0 reduce-scatter.4.cloned.1.call-update
  93.6 31.6 %reduce-scatter.4.cloned.1.call-done = f32[1280,1]{1,0:T(8,128)} async-done(((f32[5120,1]{1,0:T(8,128)}), f32[1280,1]{1,0:T(8,128)}) %reduce-scatter.4.cloned.1.call-update) | async-done | bytes 5136
  125.3 1.9 %copy.11 = bf16[1,1280]{1,0:T(2,128)(2,1)} copy(f32[1,1280]{0,1:T(8,128)} %bitcast.41) | data formatting | bytes 7680
  (3 shorter events, 0.1 us)
Async XLA Ops:
  41.0 12.2 %all-to-all-start.1 = ((f32[1,32,2,8]{3,2,0,1:T(2,128)}), f32[1,32,2,8]{3,2,0,1:T(2,128)S(1)}, u32[]{:S(2)}, u32[]{:S(2)}) async-start(f32[1,32,2,8]{3,2,0,1:T(2,128)} %bitcast.3), calls=%async_computation.1 | async-start | bytes 65536 | tf_op jit(solution)/shard_map/all_to_all | solution.py:24
  53.1 11.3 %all-to-all-start.2 = ((f32[1,32,2,8]{3,2,0,1:T(2,128)}), f32[1,32,2,8]{3,2,0,1:T(2,128)S(1)}, u32[]{:S(2)}, u32[]{:S(2)}) async-start(f32[1,32,2,8]{3,2,0,1:T(2,128)} %bitcast.5), calls=%async_computation.2 | async-start | bytes 65536 | tf_op jit(solution)/shard_map/all_to_all | solution.py:25
  64.4 15.6 %all-to-all-start = ((f32[1,32,2,8,128]{4,3,2,0,1:T(8,128)}), f32[1,32,2,8,128]{4,3,2,0,1:T(8,128)S(1)}, u32[]{:S(2)}, u32[]{:S(2)}) async-start(f32[1,32,2,8,128]{4,3,2,0,1:T(8,128)} %convolution_bitcast_fusion), calls=%async_computation | async-start | bytes 524288 | tf_op jit(solution)/shard_map/all_to_all | solution.py:26
  71.1 54.2 %reduce-scatter.4.cloned.1.call-start = ((), (), s32[]{:S(2)}) async-start(), calls=%async_computation.4 | async-start | bytes 3276800
Sparse Core Ops, SparseCore 0:
  93.8 31.4 reduce-scatter.3
where the time goes:
time: 135 us; the launch traced here: 134 us
  waiting for transfers between devices  46.7 us (35%)
  blocking collectives  27.3 us (20%)
  matrix products  26.3 us (19%)
  starting transfers between devices  15.5 us (11%)
  between operations  13.4 us (10%)
  other arithmetic  2.83 us (2%)
  local copies, waits for them, and re-layouts  1.91 us (1%)
    unnamed x2, waiting for transfers between devices  31.6 us
    all_gather x1, blocking collectives, per_device(): all_queries = lax.all_gather(new_queries, 'seq', axis=0, tiled=True)  27.3 us
    dot_general x1, matrix products, per_device(): jnp.einsum('bkgd,kgdm->bm', read, out_weight, preferred_element_type=jnp....  13.4 us
    all_to_all x1, waiting for transfers between devices, per_device(): lax.all_to_all(read_sum[None], 'seq', split_axis=1, concat_axis=0, tiled=...  8.74 us
    all_to_all x1, starting transfers between devices, per_device(): lax.all_to_all(read_sum[None], 'seq', split_axis=1, concat_axis=0, tiled=...  6.68 us
    dot_general x1, matrix products, per_device(): jnp.einsum('bkgt,bktd->bkgd', part, stored_values.astype(jnp.float32), pr...  6.5 us
    dot_general x1, matrix products, per_device(): jnp.einsum('bkgd,bktd->bkgt', all_queries, stored_keys, preferred_element...  6.36 us
    all_to_all x1, waiting for transfers between devices, per_device(): lax.all_to_all(top[None], 'seq', split_axis=1, concat_axis=0, tiled=True)  5.49 us
  transfers between devices with their start and end apart: 4, of which 4 were waited for; matrix products, arithmetic and copies ran while one was open for 6% of the time, Pallas kernels for 0%

commit v1 on v0

--- a/solution.py
+++ b/solution.py
@@ -7,7 +7,9 @@
 
 
 def per_device(new_queries, stored_keys, stored_values, used_length, out_weight):
-    all_queries = lax.all_gather(new_queries, "seq", axis=0, tiled=True)
+    all_queries = jnp.concatenate(
+        lax.all_to_all(jnp.stack([new_queries] * lax.axis_size("seq")), "seq", 0, 0), axis=0
+    )
     logit = jnp.einsum(
         "bkgd,bktd->bkgt", all_queries, stored_keys, preferred_element_type=jnp.float32
     ) * HEAD_SIZE ** (-0.5)

time: 135 us -> 124 us (0.919)
  blocking collectives: 27.3 us -> 0 us
  starting transfers between devices: 15.5 us -> 23.9 us
  waiting for transfers between devices: 46.7 us -> 53.7 us
    all_gather x1 -> x0, blocking collectives: 27.3 us -> none  [per_device(): all_queries = lax.all_gather(new_queries, 'seq', axis=0, tiled=True)]
    all_to_all x0 -> x1, starting transfers between devices: none -> 9.42 us  [per_device(): lax.all_to_all(jnp.stack([new_queries] * lax.axis_size('seq')), 'seq', 0, 0)]
    all_to_all x0 -> x1, waiting for transfers between devices: none -> 6.84 us  [per_device(): lax.all_to_all(jnp.stack([new_queries] * lax.axis_size('seq')), 'seq', 0, 0)]
  transfers between devices with their start and end apart: 4 -> 5, of which waited for: 4 -> 5; matrix products, arithmetic and copies ran while one was open for 6% -> 7% of each run, Pallas kernels for 0% -> 0%
where the time goes in v1:
time: 124 us; the launch traced here: 123 us
  waiting for transfers between devices  53.7 us (43%)
  matrix products  26.3 us (21%)
  starting transfers between devices  23.9 us (19%)
  between operations  13.5 us (11%)
  local copies, waits for them, and re-layouts  3.25 us (3%)
  other arithmetic  2.84 us (2%)
    unnamed x2, waiting for transfers between devices  31.6 us
    dot_general x1, matrix products, per_device(): jnp.einsum('bkgd,kgdm->bm', read, out_weight, preferred_element_type=jnp....  13.4 us
    all_to_all x1, starting transfers between devices, per_device(): lax.all_to_all(jnp.stack([new_queries] * lax.axis_size('seq')), 'seq', 0, 0)  9.42 us
    all_to_all x1, waiting for transfers between devices, per_device(): lax.all_to_all(read_sum[None], 'seq', split_axis=1, concat_axis=0, tiled=...  8.74 us
    all_to_all x1, waiting for transfers between devices, per_device(): lax.all_to_all(jnp.stack([new_queries] * lax.axis_size('seq')), 'seq', 0, 0)  6.84 us
    all_to_all x1, starting transfers between devices, per_device(): lax.all_to_all(read_sum[None], 'seq', split_axis=1, concat_axis=0, tiled=...  6.69 us
    dot_general x1, matrix products, per_device(): jnp.einsum('bkgt,bktd->bkgd', part, stored_values.astype(jnp.float32), pr...  6.5 us
    dot_general x1, matrix products, per_device(): jnp.einsum('bkgd,bktd->bkgt', all_queries, stored_keys, preferred_element...  6.36 us
  transfers between devices with their start and end apart: 5, of which 5 were waited for; matrix products, arithmetic and copies ran while one was open for 7% of the time, Pallas kernels for 0%

profile of v1, /device:TPU:1, one launch (start us, length us, event | category | flops | bytes accessed | tf_op | source)
XLA Modules:
  0.0 123.4 jit_solution(12774483349527996605)
XLA Ops:
  6.5 1.3 %stack.2 = bf16[32,1,2,8,128]{4,3,2,1,0:T(8,128)(2,1)} broadcast(bf16[2,8,128]{2,1,0:T(8,128)(2,1)} %bitcast.47), dimensions={2,3,4} | broadcast | bytes 135168 | tf_op jit(solution)/shard_map/stack | solution.py:11
  7.9 9.4 %all-to-all-start = ((bf16[32,1,2,8,128]{4,3,2,1,0:T(8,128)(2,1)}), bf16[32,1,2,8,128]{4,3,2,1,0:T(8,128)(2,1)S(1)}, u32[]{:S(2)}, u32[]{:S(2)}) async-start(bf16[32,1,2,8,128]{4,3,2,1,0:T(8,128)(2,1)} %stack.2), calls=%async_computation | async-start | bytes 262144 | tf_op jit(solution)/shard_map/all_to_all | solution.py:11
  17.3 0.7 broadcast_compare_fusion
  18.1 6.8 %all-to-all-done = bf16[32,1,2,8,128]{4,3,2,1,0:T(8,128)(2,1)S(1)} async-done(((bf16[32,1,2,8,128]{4,3,2,1,0:T(8,128)(2,1)}), bf16[32,1,2,8,128]{4,3,2,1,0:T(8,128)(2,1)S(1)}, u32[]{:S(2)}, u32[]{:S(2)}) %all-to-all-start) | async-done | bytes 131104 | tf_op jit(solution)/shard_map/all_to_all | solution.py:11
  24.9 6.4 %fusion.19 = (f32[32,2,8]{2,1,0:T(2,128)}, f32[32,2,8,512]{3,2,1,0:T(8,128)S(1)}) fusion(bf16[32,2,512,128]{3,2,1,0:T(8,128)(2,1)} %param.6, bf16[32,1,2,8,128]{4,3,2,1,0:T(8,128)(2,1)S(1)} %all-to-all-done, pred[32,512]{1,0:T(8,128)(4,1)S(1)} %broadcast_compare_fusion), kind=kOutput, calls=%fused_computation.26 | convolution fusion | flops 67894784 | bytes 9586688 | tf_op jit(solution)/shard_map/bkgd,bktd->bkgt/dot_general | solution.py:13
  31.3 3.9 %all-to-all-start.2 = ((f32[1,32,2,8]{3,2,0,1:T(2,128)}), f32[1,32,2,8]{3,2,0,1:T(2,128)S(1)}, u32[]{:S(2)}, u32[]{:S(2)}) async-start(f32[1,32,2,8]{3,2,0,1:T(2,128)} %bitcast.5), calls=%async_computation.2 | async-start | bytes 65536 | tf_op jit(solution)/shard_map/all_to_all | solution.py:26
  35.2 1.8 %fusion.6 = f32[32,2,8]{2,1,0:T(2,128)} fusion(f32[32,2,8,512]{3,2,1,0:T(8,128)S(1)} %get-tuple-element.6, f32[32,2,8]{2,1,0:T(2,128)} %get-tuple-element.5, pred[32,512]{1,0:T(8,128)(4,1)S(1)} %broadcast_compare_fusion), kind=kLoop, calls=%fused_computation.7 | loop fusion | flops 785920 | bytes 1069056 | tf_op jit(solution)/shard_map/reduce_sum | solution.py:21
  36.9 5.6 %all-to-all-done.2 = f32[1,32,2,8]{3,2,0,1:T(2,128)S(1)} async-done(((f32[1,32,2,8]{3,2,0,1:T(2,128)}), f32[1,32,2,8]{3,2,0,1:T(2,128)S(1)}, u32[]{:S(2)}, u32[]{:S(2)}) %all-to-all-start.2) | async-done | bytes 2080 | tf_op jit(solution)/shard_map/all_to_all | solution.py:26
  42.5 3.9 %all-to-all-start.3 = ((f32[1,32,2,8]{3,2,0,1:T(2,128)}), f32[1,32,2,8]{3,2,0,1:T(2,128)S(1)}, u32[]{:S(2)}, u32[]{:S(2)}) async-start(f32[1,32,2,8]{3,2,0,1:T(2,128)} %bitcast.7), calls=%async_computation.3 | async-start | bytes 65536 | tf_op jit(solution)/shard_map/all_to_all | solution.py:27
  46.4 6.5 %convolution_bitcast_fusion = f32[1,32,2,8,128]{4,3,2,0,1:T(8,128)} fusion(bf16[32,2,512,128]{3,2,1,0:T(8,128)(2,1)} %param.7, f32[32,2,8,512]{3,2,1,0:T(8,128)S(1)} %get-tuple-element.6, f32[32,2,8]{2,1,0:T(2,128)} %get-tuple-element.5, pred[32,512]{1,0:T(8,128)(4,1)S(1)} %broadcast_compare_fusion), kind=kOutput, calls=%fused_computation.5 | convolution fusion | flops 403177472 | bytes 9717760 | tf_op jit(solution)/shard_map/bkgt,bktd->bkgd/dot_general | solution.py:22
  53.0 0.8 all-to-all-done.3
  53.8 6.7 %all-to-all-start.1 = ((f32[1,32,2,8,128]{4,3,2,0,1:T(8,128)}), f32[1,32,2,8,128]{4,3,2,0,1:T(8,128)S(1)}, u32[]{:S(2)}, u32[]{:S(2)}) async-start(f32[1,32,2,8,128]{4,3,2,0,1:T(8,128)} %convolution_bitcast_fusion), calls=%async_computation.1 | async-start | bytes 524288 | tf_op jit(solution)/shard_map/all_to_all | solution.py:28
  60.5 0.0 reduce-scatter.4.cloned.1.call-start
  60.5 0.1 fusion.15
  60.6 8.7 %all-to-all-done.1 = f32[1,32,2,8,128]{4,3,2,0,1:T(8,128)S(1)} async-done(((f32[1,32,2,8,128]{4,3,2,0,1:T(8,128)}), f32[1,32,2,8,128]{4,3,2,0,1:T(8,128)S(1)}, u32[]{:S(2)}, u32[]{:S(2)}) %all-to-all-start.1) | async-done | bytes 262176 | tf_op jit(solution)/shard_map/all_to_all | solution.py:28
  69.4 0.1 fusion.10
  69.5 0.1 fusion.17
  69.6 13.4 %fusion.2 = f32[5120,1]{1,0:T(8,128)} fusion(bf16[2,8,128,5120]{3,2,1,0:T(8,128)(2,1)} %param.9, bf16[2,8,128,1]{2,1,0,3:T(8,128)(2,1)S(1)} %fusion.17), kind=kOutput, calls=%fused_computation.2 | convolution fusion | flops 20971520 | bytes 20996096 | tf_op jit(solution)/shard_map/bkgd,kgdm->bm/dot_general | solution.py:35
  83.0 0.0 reduce-scatter.4.cloned.1.call-update
  83.0 31.6 %reduce-scatter.4.cloned.1.call-done = f32[1280,1]{1,0:T(8,128)} async-done(((f32[5120,1]{1,0:T(8,128)}), f32[1280,1]{1,0:T(8,128)}) %reduce-scatter.4.cloned.1.call-update) | async-done | bytes 5136
  114.7 1.9 %copy.11 = bf16[1,1280]{1,0:T(2,128)(2,1)} copy(f32[1,1280]{0,1:T(8,128)} %bitcast.46) | data formatting | bytes 7680
  (3 shorter events, 0.1 us)
Async XLA Ops:
  7.9 17.0 %all-to-all-start = ((bf16[32,1,2,8,128]{4,3,2,1,0:T(8,128)(2,1)}), bf16[32,1,2,8,128]{4,3,2,1,0:T(8,128)(2,1)S(1)}, u32[]{:S(2)}, u32[]{:S(2)}) async-start(bf16[32,1,2,8,128]{4,3,2,1,0:T(8,128)(2,1)} %stack.2), calls=%async_computation | async-start | bytes 262144 | tf_op jit(solution)/shard_map/all_to_all | solution.py:11
  31.3 11.3 %all-to-all-start.2 = ((f32[1,32,2,8]{3,2,0,1:T(2,128)}), f32[1,32,2,8]{3,2,0,1:T(2,128)S(1)}, u32[]{:S(2)}, u32[]{:S(2)}) async-start(f32[1,32,2,8]{3,2,0,1:T(2,128)} %bitcast.5), calls=%async_computation.2 | async-start | bytes 65536 | tf_op jit(solution)/shard_map/all_to_all | solution.py:26
  42.5 11.3 %all-to-all-start.3 = ((f32[1,32,2,8]{3,2,0,1:T(2,128)}), f32[1,32,2,8]{3,2,0,1:T(2,128)S(1)}, u32[]{:S(2)}, u32[]{:S(2)}) async-start(f32[1,32,2,8]{3,2,0,1:T(2,128)} %bitcast.7), calls=%async_computation.3 | async-start | bytes 65536 | tf_op jit(solution)/shard_map/all_to_all | solution.py:27
  53.8 15.6 %all-to-all-start.1 = ((f32[1,32,2,8,128]{4,3,2,0,1:T(8,128)}), f32[1,32,2,8,128]{4,3,2,0,1:T(8,128)S(1)}, u32[]{:S(2)}, u32[]{:S(2)}) async-start(f32[1,32,2,8,128]{4,3,2,0,1:T(8,128)} %convolution_bitcast_fusion), calls=%async_computation.1 | async-start | bytes 524288 | tf_op jit(solution)/shard_map/all_to_all | solution.py:28
  60.5 54.2 %reduce-scatter.4.cloned.1.call-start = ((), (), s32[]{:S(2)}) async-start(), calls=%async_computation.5 | async-start | bytes 3276800
Sparse Core Ops, SparseCore 0:
  83.2 31.4 reduce-scatter.3
